TPU v7x, 8 devices: a whole 2x2x1 slice. The times are simulated.
8 devices in a mesh: dp: 1 (over z), sp: 2 (over y), cp: 4 (over x, core).
Axes of the slice: x: 2, y: 2, z: 1, core: 2. Of those that a mesh axis runs over, the one named last changes fastest.
Arguments:
- x_act: bfloat16 [32, 96, 14, 1024], P('dp', 'sp', None, 'cp')
- w_one: bfloat16 [3, 3, 1024, 4096], P(None, None, 'cp')
- w_two: bfloat16 [3, 3, 4096, 1024], P(None, None, 'cp')
- bias_one: float32 [4096], replicated
Outputs:
- output: bfloat16 [32, 96, 14, 1024], P('dp', 'sp', None, 'cp')
All inputs are finite; a program needn't handle non-finite values.
Results may differ from a plain program's by a relative error of at most 0.001.
Values are sent between devices in bfloat16 or wider.
A program may use at most 1 GiB of HBM per device.

v0:
```python
import jax
import jax.numpy as jnp
from jax import lax
from jax.sharding import PartitionSpec as P, NamedSharding

CONV_DIMS = ("NHWC", "HWIO", "NHWC")


def solution(mesh):
    row_devs = mesh.shape["sp"]
    down_perm = [(src_dev, src_dev + 1) for src_dev in range(row_devs - 1)]
    up_perm = [(src_dev + 1, src_dev) for src_dev in range(row_devs - 1)]
    act_spec = P("dp", "sp", None, "cp")
    kernel_spec = P(None, None, "cp", None)

    def with_halo(act_tile):
        from_above = lax.ppermute(act_tile[:, -1:], "sp", down_perm)
        from_below = lax.ppermute(act_tile[:, :1], "sp", up_perm)
        return jnp.concatenate([from_above, act_tile, from_below], axis=1)

    def conv_rows(padded, kernel):
        return lax.conv_general_dilated(padded, kernel, (1, 1), ((0, 0), (1, 1)), dimension_numbers=CONV_DIMS, preferred_element_type=jnp.float32)

    def local_block(x_tile, w_one_part, w_two_part, bias_part):
        part_one = conv_rows(with_halo(x_tile), w_one_part)
        summed_one = lax.psum_scatter(part_one, "cp", scatter_dimension=3, tiled=True)
        hidden = jax.nn.relu(summed_one + bias_part).astype(jnp.bfloat16)
        part_two = conv_rows(with_halo(hidden), w_two_part)
        summed_two = lax.psum_scatter(part_two, "cp", scatter_dimension=3, tiled=True)
        return (x_tile.astype(jnp.float32) + summed_two).astype(jnp.bfloat16)

    return jax.shard_map(local_block, mesh=mesh, in_specs=(act_spec, kernel_spec, kernel_spec, P("cp")), out_specs=act_spec, check_vma=False)
```

profile of v0, /device:TPU:0, one launch (start us, length us, event | category | flops | bytes accessed | tf_op | source)
XLA Modules:
  0.0 3798.4 jit_solution(13171366539351568131)
XLA Ops:
  6.5 0.0 reduce-scatter.3.cloned.1.call-start
  6.5 8.2 copy.5
  14.7 5.3 collective-permute-start
  20.0 1.3 collective-permute-start.1
  21.3 3.5 collective-permute-done
  24.8 4.1 collective-permute-done.1
  29.0 5.8 fusion.24
  34.8 425.5 %fusion.6 = f32[32,48,14,4096]{3,0,2,1:T(8,128)} fusion(bf16[3,3,256,4096]{3,2,1,0:T(8,128)(2,1)} %param.5, bf16[32,50,14,256]{3,0,2,1:T(8,128)(2,1)} %fusion.24), kind=kOutput, calls=%fused_computation.8 | convolution fusion | flops 386547056640 | bytes 382664704 | tf_op jit(solution)/shard_map/conv_general_dilated | solution.py:22
  460.3 0.0 copy-start
  460.3 0.0 reduce-scatter.3.cloned.1.call-update
  460.3 0.0 reduce-scatter.5.cloned.1.call-start
  460.4 0.6 copy-done
  461.0 0.6 dynamic-slice
  462.2 0.7 dynamic-slice.2
  462.9 2224.1 %reduce-scatter.3.cloned.1.call-done = f32[32,48,14,1024]{3,0,2,1:T(8,128)} async-done(((f32[32,48,14,4096]{3,0,2,1:T(8,128)}), f32[32,48,14,1024]{3,0,2,1:T(8,128)}) %reduce-scatter.3.cloned.1.call-update) | async-done | bytes 88080400 | tf_op jit(solution)/shard_map/reduce_scatter | solution.py:26
  2687.0 43.3 %maximum_convert_fusion = bf16[32,48,14,1024]{3,0,2,1:T(8,128)(2,1)} fusion(f32[32,48,14,1024]{3,0,2,1:T(8,128)} %reduce-scatter.3.cloned.1.call-done, f32[1024]{0:T(1024)S(1)} %dynamic-slice.2), kind=kLoop, calls=%fused_computation | loop fusion | flops 66060288 | bytes 132124672 | tf_op jit(solution)/shard_map/convert_element_type | solution.py:27
  2730.3 1.6 fusion.14
  2731.9 3.4 collective-permute-start.2
  2735.4 1.3 collective-permute-start.3
  2736.7 18.0 collective-permute-done.2
  2754.6 4.2 collective-permute-done.3
  2758.8 438.4 %fusion = f32[32,48,14,1024]{3,0,2,1:T(8,128)} fusion(bf16[3,3,1024,1024]{3,2,1,0:T(8,128)(2,1)} %param.6, bf16[32,1,14,1024]{3,0,2,1:T(8,128)(2,1)S(1)} %collective-permute-done.3, bf16[32,48,14,1024]{3,0,2,1:T(8,128)(2,1)} %maximum_convert_fusion, bf16[32,1,14,1024]{3,0,2,1:T(8,128)(2,1)S(1)} %collective-permute-done.2), kind=kOutput, calls=%fused_computation.1 | convolution fusion | flops 386684682240 | bytes 152829952 | tf_op jit(solution)/shard_map/conv_general_dilated | solution.py:22
  3197.2 0.0 reduce-scatter.5.cloned.1.call-update
  3197.3 564.7 %reduce-scatter.5.cloned.1.call-done = f32[32,48,14,256]{3,0,2,1:T(8,128)} async-done(((f32[32,48,14,1024]{3,0,2,1:T(8,128)}), f32[32,48,14,256]{3,0,2,1:T(8,128)}) %reduce-scatter.5.cloned.1.call-update) | async-done | bytes 22020112 | tf_op jit(solution)/shard_map/reduce_scatter | solution.py:29
  3762.0 12.1 add_convert_fusion
  3774.1 17.1 copy.9
  (1 shorter events, 0.0 us)
Async XLA Ops:
  6.5 2680.5 %reduce-scatter.3.cloned.1.call-start = ((), (), s32[]{:S(2)}) async-start(), calls=%async_computation.2 | async-start | bytes 440401920 | tf_op jit(solution)/shard_map/reduce_scatter | solution.py:26
  14.7 10.1 collective-permute-start
  20.0 9.0 collective-permute-start.1
  460.3 0.7 copy-start
  460.3 3301.7 %reduce-scatter.5.cloned.1.call-start = ((), (), s32[]{:S(2)}) async-start(), calls=%async_computation.3 | async-start | bytes 110100480 | tf_op jit(solution)/shard_map/reduce_scatter | solution.py:29
  2731.9 22.7 collective-permute-start.2
  2735.4 23.5 collective-permute-start.3
Sparse Core Ops, SparseCore 0:
  460.5 2226.4 reduce-scatter.2
  3197.4 564.5 reduce-scatter.4
where the time goes:
time: 3810 us; the launch traced here: 3800 us
  waiting for transfers between devices  2820 us (74%)
  matrix products  864 us (23%)
  other arithmetic  61.3 us (2%)
    reduce_scatter x1, waiting for transfers between devices, local_block(): lax.psum_scatter(part_one, 'cp', scatter_dimension=3, tiled=True)  2220 us
    conv_general_dilated x2, matrix products, conv_rows(): lax.conv_general_dilated(padded, kernel, (1, 1), ((0, 0), (1, 1)), dimens...  864 us
    reduce_scatter x1, waiting for transfers between devices, local_block(): lax.psum_scatter(part_two, 'cp', scatter_dimension=3, tiled=True)  565 us
  transfers between devices with their start and end apart: 6, of which 6 were waited for; matrix products, arithmetic and copies ran while one was open for 0% of the time, Pallas kernels for 0%

commit v1 on v0

v1 whole, which is shorter than its diff:
```python
import functools

import jax
import jax.numpy as jnp
from jax import lax
from jax.experimental import pallas as pl
from jax.experimental.pallas import tpu as pltpu
from jax.sharding import PartitionSpec as P

MESH = pl.DeviceIdType.MESH
N_STEPS = 64


def fused_block(xt, w_one, w_two, bias):
    groups, h_loc, cols, ni, cb = xt.shape
    rows = h_loc // 2
    m_rows = rows * ni
    tile = 2 * cb

    def remote(src, dst, send_sem, recv_sem, sp, cp):
        return pltpu.make_async_remote_copy(src_ref=src, dst_ref=dst, send_sem=send_sem, recv_sem=recv_sem,
                                            device_id={"sp": sp, "cp": cp}, device_id_type=MESH)

    def kernel(xt, w1, w2, b1, yt, g1, g2, part, hid,
               xa, acc, wv, stage,
               wsem, asem, pst, pld, stl, zsem, xl, xs, xr, hs, hr,
               p1s, p1r, x1s, x1r, y1s, y1r, f1s, f1r,
               p2s, p2r, x2s, x2r, y2s, y2r, f2s, f2r,
               as_, ar, ys, yr, zs, zr, yl):
        sp = lax.axis_index("sp")
        k = lax.axis_index("cp")
        x = lax.div(k, 2)
        c = lax.rem(k, 2)
        blk = 2 * sp + c
        osp = 1 - sp
        k1 = 2 * x + (1 - c)
        k2 = 2 * (1 - x) + c
        k3 = 2 * (1 - x) + (1 - c)

        def tile_of(xx, j, par):
            return 4 * lax.rem(xx + lax.div(j, 2), 2) + 2 * lax.rem(j, 2) + par

        barrier = pltpu.get_barrier_semaphore()
        for d_sp in range(2):
            for d_cp in range(4):
                if d_sp or d_cp:
                    pl.semaphore_signal(barrier, inc=1, device_id={"sp": lax.rem(sp + d_sp, 2), "cp": lax.rem(k + d_cp, 4)},
                                        device_id_type=MESH)
        pl.semaphore_wait(barrier, 7)

        def x_copy(role):
            cc = c if role in (0, 2) else 1 - c
            xx = x if role < 2 else 1 - x
            src = xt.at[xx, pl.ds((rows - 1) * cc, rows + 1)]
            dst = xa.at[role, pl.ds(1 - cc, rows + 1)]
            if role == 0:
                return pltpu.make_async_copy(src, dst, xl.at[0])
            return remote(src, dst, xs.at[role - 1], xr.at[role - 1], sp, {1: k1, 2: k2, 3: k3}[role])

        def halo_copy(xx):
            role = 2 * lax.rem(x + xx, 2) + lax.rem(c + sp, 2)
            return remote(xt.at[xx, (h_loc - 1) * osp], xa.at[role, (rows + 1) * sp], hs.at[xx], hr.at[role], osp, 2 * xx + sp)

        half = cb // 2

        def w1_own(j, par, xx):
            return w1.at[:, :, :, pl.ds(pl.multiple_of(tile_of(xx, j, par) * tile, tile), tile)]

        def w1_part(j, par):
            return remote(w1_own(j, par, x), g1.at[0, j, par], p1s.at[j, par], p1r.at[j, par], sp, k1)

        def w1_x(j, hf):
            cut = pl.ds(pl.multiple_of(hf * half, half), half)
            src = w1.at[:, :, cut, pl.ds(pl.multiple_of(tile_of(1 - x, j, sp) * tile, tile), tile)]
            return remote(src, g1.at[1, j, sp, :, :, cut], x1s.at[j, hf], x1r.at[j, hf], sp, k2)

        def w1_y(j, hf):
            cut = pl.ds(pl.multiple_of(hf * half, half), half)
            ref = g1.at[1, j, sp, :, :, cut]
            return remote(ref, ref, y1s.at[j, hf], y1r.at[j, hf], osp, k)

        def w1_fwd(j, par, hf):
            cut = pl.ds(pl.multiple_of(hf * half, half), half)
            return remote(g1.at[1, j, par, :, :, cut], g1.at[2, j, par, :, :, cut], f1s.at[j, par, hf], f1r.at[j, par, hf], sp, k1)

        def w2_cut(n, par, h, xx):
            row = pl.multiple_of(par * tile + h * cb, cb)
            col = pl.multiple_of(tile * lax.rem(1 + xx + n, 2), tile)
            return w2.at[:, :, pl.ds(row, cb), pl.ds(col, tile)]

        def w2_part(n, par, h):
            return remote(w2_cut(n, par, h, x), g2.at[0, n, par, h], p2s.at[n, par, h], p2r.at[n, par, h], sp, k1)

        def w2_x(n, h):
            return remote(w2_cut(n, sp, h, 1 - x), g2.at[1, n, sp, h], x2s.at[n, h], x2r.at[n, h], sp, k2)

        def w2_y(n, h):
            ref = g2.at[1, n, sp, h]
            return remote(ref, ref, y2s.at[n, h], y2r.at[n, h], osp, k)

        def w2_fwd(n, par, h):
            return remote(g2.at[1, n, par, h], g2.at[2, n, par, h], f2s.at[n, par, h], f2r.at[n, par, h], sp, k1)

        up_blk = lax.max(blk - 1, 0)
        dn_blk = lax.min(blk + 1, 3)

        def hid_up(q, h):
            return remote(stage.at[h, 0], hid.at[q, rows + 1], as_.at[0, h], ar.at[1, q], lax.div(up_blk, 2), 2 * x + lax.rem(up_blk, 2))

        def hid_dn(q, h):
            return remote(stage.at[h, rows - 1], hid.at[q, 0], as_.at[1, h], ar.at[0, q], lax.div(dn_blk, 2), 2 * x + lax.rem(dn_blk, 2))

        def hid_store(q, h):
            return pltpu.make_async_copy(stage.at[h], hid.at[q, pl.ds(1, rows)], stl.at[h])

        y_rows = pl.ds(rows * c, rows)

        def y_far(h):
            return remote(stage.at[h], yt.at[x, y_rows], ys.at[h], yr.at[lax.rem(h + c, 2)], sp, 2 * (1 - x) + h)

        def y_near():
            return remote(stage.at[1 - c], yt.at[x, y_rows], zs.at[0], zr.at[0], sp, k1)

        def y_own():
            return pltpu.make_async_copy(stage.at[c], yt.at[x, y_rows], yl.at[0])

        def zero_rows(row):
            return pltpu.make_async_copy(stage.at[0, pl.ds(0, 16)], hid.at[:, row], zsem.at[0])

        x_copy(0).start()
        for xx in range(2):
            halo_copy(xx).start()
        x_copy(1).start()

        def p_of(m):
            return lax.rem(m + 2, 8)

        def jp(p):
            return lax.div(p, 2), lax.rem(sp + lax.rem(p, 2), 2)

        for m in range(3):
            w1_part(*jp(jnp.int32((m + 2) % 8))).start()
        for hf in range(2):
            w1_x(0, hf).start()

        stage[0, 0:16] = jnp.zeros((16, cols, ni, cb), jnp.bfloat16)

        @pl.when(blk == 0)
        def _():
            xa[0:4, 0] = jnp.zeros((4, cols, ni, cb), jnp.bfloat16)
            zero_rows(0).start()

        @pl.when(blk == 3)
        def _():
            xa[0:4, rows + 1] = jnp.zeros((4, cols, ni, cb), jnp.bfloat16)
            zero_rows(rows + 1).start()

        def w_load(src, t):
            return pltpu.make_async_copy(src, wv.at[lax.rem(t, 2)], wsem.at[lax.rem(t, 2)])

        def hid_load(a, q):
            slot = lax.rem(q, 2)
            return pltpu.make_async_copy(hid.at[a], xa.at[4 + slot], asem.at[slot])

        def issue(t):
            @pl.when(t < 16)
            def _():
                j, par = jp(p_of(lax.div(t, 2)))

                @pl.when(lax.rem(t, 2) == 0)
                def _():
                    w_load(w1_own(j, par, x), t).start()

                @pl.when(lax.rem(t, 2) == 1)
                def _():
                    w1_part(j, par).wait_recv()
                    w_load(g1.at[0, j, par], t).start()

            @pl.when((t >= 16) & (t < 32))
            def _():
                j, par = jp(lax.div(t - 16, 2))

                @pl.when(lax.rem(t, 2) == 1)
                def _():
                    for hf in range(2):
                        w1_fwd(j, par, hf).wait_recv()

                w_load(g1.at[1 + lax.rem(t, 2), j, par], t).start()

            @pl.when((t >= 32) & (t < N_STEPS))
            def _():
                n = lax.div(t - 32, 16)
                q = lax.rem(t - 32, 16)
                h = lax.rem(q, 2)
                p = lax.div(q, 2)
                j, par = jp(p)
                a = 4 * j + 2 * par + h
                same = lax.rem(j, 2) == c

                @pl.when((n == 0) & (blk > 0))
                def _():
                    hid_dn(a, h).wait_recv()

                @pl.when((n == 0) & (blk < 3))
                def _():
                    hid_up(a, h).wait_recv()

                hid_load(a, q).start()

                @pl.when((p < 4) & same)
                def _():
                    w_load(w2_cut(n, par, h, x), t).start()

                @pl.when((p < 4) & jnp.logical_not(same))
                def _():
                    w2_part(n, par, h).wait_recv()
                    w_load(g2.at[0, n, par, h], t).start()

                @pl.when((p >= 4) & same)
                def _():
                    w_load(g2.at[1, n, par, h], t).start()

                @pl.when((p >= 4) & jnp.logical_not(same))
                def _():
                    w2_fwd(n, par, h).wait_recv()
                    w_load(g2.at[2, n, par, h], t).start()

        issue(jnp.int32(0))
        x_copy(0).wait()

        @pl.when(c != sp)
        def _():
            for role in range(4):
                remote(xt.at[0, 0], xa.at[role, 0], hs.at[0], hr.at[role], osp, k).wait_recv()

        def events(i):
            @pl.when((lax.rem(i, 2) == 0) & (i < 10))
            def _():
                w1_part(*jp(p_of(lax.div(i, 2) + 3))).start()

            @pl.when(i == 1)
            def _():
                x_copy(1).wait_recv()

            @pl.when(i == 3)
            def _():
                x_copy(2).start()

            @pl.when(i == 7)
            def _():
                x_copy(3).start()

            @pl.when((i == 13) | (i == 17) | (i == 21))
            def _():
                j = lax.div(i - 8, 4)
                for hf in range(2):
                    w1_x(j, hf).start()

            @pl.when((i == 24) | (i == 28) | (i == 32) | (i == 36))
            def _():
                e = lax.div(i - 24, 4)
                w2_x(lax.div(e, 2), lax.rem(e, 2)).start()

            @pl.when((i >= 18) & (i < 26))
            def _():
                e = i - 18
                w2_part(lax.div(e, 4), lax.rem(lax.div(e, 2), 2), lax.rem(e, 2)).start()

            @pl.when(i == 6)
            def _():
                for hf in range(2):
                    w1_x(0, hf).wait_recv()
                    w1_y(0, hf).start()
                    w1_fwd(0, sp, hf).start()

            @pl.when((i >= 17) & (i < 28) & (lax.rem(i, 2) == 1))
            def _():
                e = lax.div(i - 13, 2)
                j = lax.div(e, 2)
                hf = lax.rem(e, 2)
                w1_x(j, hf).wait_recv()
                w1_y(j, hf).start()
                w1_fwd(j, sp, hf).start()

            @pl.when((i == 31) | (i == 35) | (i == 39) | (i == 44))
            def _():
                e = lax.div(i - 31, 4)
                w2_x(lax.div(e, 2), lax.rem(e, 2)).wait_recv()
                w2_y(lax.div(e, 2), lax.rem(e, 2)).start()
                w2_fwd(lax.div(e, 2), sp, lax.rem(e, 2)).start()

            @pl.when(i == 11)
            def _():
                for hf in range(2):
                    w1_y(0, hf).wait_recv()
                    w1_fwd(0, osp, hf).start()

            @pl.when((i == 20) | (i == 24) | (i == 28))
            def _():
                j = lax.div(i - 16, 4)
                w1_y(j, 0).wait_recv()
                w1_fwd(j, osp, 0).start()

            @pl.when((i == 21) | (i == 25) | (i == 29))
            def _():
                j = lax.div(i - 17, 4)
                w1_y(j, 1).wait_recv()
                w1_fwd(j, osp, 1).start()

            @pl.when((i == 36) | (i == 40) | (i == 45) | (i == 49))
            def _():
                e = lax.div(i - 36, 4)
                w2_y(lax.div(e, 2), lax.rem(e, 2)).wait_recv()
                w2_fwd(lax.div(e, 2), osp, lax.rem(e, 2)).start()

            stored = (i >= 19) & (i <= 33) & (lax.rem(i, 2) == 1)

            @pl.when(stored)
            def _():
                for h in range(2):
                    hid_store(0, h).wait()

            @pl.when(stored & (blk > 0))
            def _():
                for h in range(2):
                    hid_up(0, h).wait_send()

            @pl.when(stored & (blk < 3))
            def _():
                for h in range(2):
                    hid_dn(0, h).wait_send()

            @pl.when(i == 16)
            def _():
                x_copy(2).wait_recv()

            @pl.when(i == 17)
            def _():
                x_copy(3).wait_recv()

        def taps(xs_slot, ws_slot, col):
            total = None
            for dx in (-1, 0, 1):
                if not 0 <= col + dx < cols:
                    continue
                for dy in range(3):
                    lhs = xa[xs_slot, dy:dy + rows, col + dx].reshape(m_rows, cb)
                    prod = jnp.dot(lhs, wv[ws_slot, dy, dx + 1], preferred_element_type=jnp.float32)
                    total = prod if total is None else total + prod
            return total

        def step(i, carry):
            ph3 = i >= 32
            odd = lax.rem(i, 2) == 1
            n = jnp.where(ph3, lax.div(i - 32, 16), 0)
            q = jnp.where(ph3, lax.rem(i - 32, 16), 0)
            m = lax.div(i, 2)
            p = jnp.where(i < 16, p_of(m), lax.rem(m, 8))
            last = jnp.where(ph3, q == 15, (i >= 16) & odd)
            first = jnp.where(ph3, q == 0, (i < 16) & jnp.logical_not(odd))
            a_slot = jnp.where(ph3, n, lax.rem(p, 2))
            x_slot = jnp.where(ph3, 4 + lax.rem(q, 2), jnp.where(i < 16, 0, 2) + lax.rem(i, 2))
            w_slot = lax.rem(i, 2)

            events(i)
            issue(i + 1)
            w_load(g1.at[0, 0, 0], i).wait()

            @pl.when(ph3)
            def _():
                hid_load(0, q).wait()

            @pl.when((i >= 4) & (i < 16) & jnp.logical_not(odd))
            def _():
                pltpu.make_async_copy(acc.at[a_slot], part.at[0], pst.at[a_slot]).wait()

            @pl.when((i >= 20) & (i < 32) & jnp.logical_not(odd))
            def _():
                pltpu.make_async_copy(part.at[0], acc.at[a_slot], pld.at[a_slot]).wait()

            @pl.when(jnp.logical_not(last))
            def _():
                for col in range(cols):
                    total = taps(x_slot, w_slot, col)
                    acc[a_slot, col] = total + jnp.where(first, 0.0, acc[a_slot, col])

            @pl.when((i < 12) & odd)
            def _():
                pltpu.make_async_copy(acc.at[a_slot], part.at[p], pst.at[a_slot]).start()

            @pl.when(last)
            def _():
                @pl.when((i == 17) & ((blk == 0) | (blk == 3)))
                def _():
                    zero_rows(0).wait()

                @pl.when(i == 63)
                def _():
                    for h in range(2):
                        y_far(h).wait_send()

                keep = jnp.where(ph3, 1.0, 0.0)
                floor = jnp.where(ph3, -jnp.inf, 0.0)
                j, par = jp(p)
                shift = b1[tile_of(x, j, par)] * (1.0 - keep)
                role0 = jnp.where(n == 0, 2, 0)
                for col in range(cols):
                    total = taps(x_slot, w_slot, col) + acc[a_slot, col] + shift
                    for h in range(2):
                        role = role0 + lax.rem(c + h, 2)
                        res = xa[role, 1:rows + 1, col].reshape(m_rows, cb).astype(jnp.float32)
                        val = jnp.maximum(total[:, h * cb:(h + 1) * cb] + res * keep, floor)
                        stage[h, :, col] = val.astype(jnp.bfloat16).reshape(rows, ni, cb)

                @pl.when(i < 32)
                def _():
                    a = 4 * j + 2 * par
                    for h in range(2):
                        hid_store(a + h, h).start()

                    @pl.when(blk > 0)
                    def _():
                        for h in range(2):
                            hid_up(a + h, h).start()

                    @pl.when(blk < 3)
                    def _():
                        for h in range(2):
                            hid_dn(a + h, h).start()

                    @pl.when(p < 6)
                    def _():
                        pltpu.make_async_copy(part.at[p + 2], acc.at[a_slot], pld.at[a_slot]).start()

                @pl.when(i == 47)
                def _():
                    for h in range(2):
                        y_far(h).start()

                @pl.when(i == 63)
                def _():
                    y_near().start()
                    y_own().start()

            return carry

        lax.fori_loop(0, N_STEPS, step, 0)

        for role in range(1, 4):
            x_copy(role).wait_send()
        for xx in range(2):
            halo_copy(xx).wait_send()

        def drain(e, carry):
            hi, lo = lax.div(e, 2), lax.rem(e, 2)
            w1_part(hi, lo).wait_send()
            w1_x(hi, lo).wait_send()
            w1_y(hi, lo).wait_send()
            for hf in range(2):
                w1_fwd(hi, lo, hf).wait_send()
            n, par = lax.div(e, 4), lax.rem(lax.div(e, 2), 2)
            w2_part(n, par, lo).wait_send()
            w2_fwd(n, par, lo).wait_send()
            return carry

        lax.fori_loop(0, 8, drain, 0)

        def drain_two(e, carry):
            w2_x(lax.div(e, 2), lax.rem(e, 2)).wait_send()
            w2_y(lax.div(e, 2), lax.rem(e, 2)).wait_send()
            return carry

        lax.fori_loop(0, 4, drain_two, 0)
        for e in range(2):
            remote(stage.at[0], yt.at[0, pl.ds(0, rows)], ys.at[0], yr.at[e], sp, k).wait_recv()
        y_near().wait()
        y_own().wait()

    dma = pltpu.SemaphoreType.DMA
    bf16, f32 = jnp.bfloat16, jnp.float32
    any_space = pl.BlockSpec(memory_space=pl.ANY)
    outs = pl.pallas_call(
        kernel,
        out_shape=[
            jax.ShapeDtypeStruct(xt.shape, bf16),
            jax.ShapeDtypeStruct((3, 4, 2, 3, 3, cb, tile), bf16),
            jax.ShapeDtypeStruct((3, 2, 2, 2, 3, 3, cb, tile), bf16),
            jax.ShapeDtypeStruct((8, cols, m_rows, tile), f32),
            jax.ShapeDtypeStruct((16, rows + 2, cols, ni, cb), bf16),
        ],
        in_specs=[any_space, any_space, any_space, pl.BlockSpec(memory_space=pltpu.VMEM)],
        out_specs=[any_space] * 5,
        scratch_shapes=[
            pltpu.VMEM((6, rows + 2, cols, ni, cb), bf16),
            pltpu.VMEM((2, cols, m_rows, tile), f32),
            pltpu.VMEM((2, 3, 3, cb, tile), bf16),
            pltpu.VMEM((2, rows, cols, ni, cb), bf16),
            dma((2,)), dma((2,)), dma((2,)), dma((2,)), dma((2,)), dma((1,)), dma((1,)), dma((3,)), dma((3,)), dma((2,)), dma((4,)),
            dma((4, 2)), dma((4, 2)), dma((4, 2)), dma((4, 2)), dma((4, 2)), dma((4, 2)), dma((4, 2, 2)), dma((4, 2, 2)),
            dma((2, 2, 2)), dma((2, 2, 2)), dma((2, 2)), dma((2, 2)), dma((2, 2)), dma((2, 2)), dma((2, 2, 2)), dma((2, 2, 2)),
            dma((2, 2)), dma((2, 16)), dma((2,)), dma((2,)), dma((1,)), dma((1,)), dma((1,)),
        ],
        compiler_params=pltpu.CompilerParams(collective_id=0, has_side_effects=True, vmem_limit_bytes=60 * 1024 * 1024),
        name="fused_block",
    )(xt, w_one, w_two, bias)
    return outs[0]


def solution(mesh):
    act_spec = P("dp", "sp", None, "cp")
    kernel_spec = P(None, None, "cp", None)

    def local_block(x_tile, w_one_part, w_two_part, bias_one):
        images, h_loc, cols, cb = x_tile.shape
        ni = images // 2
        xt = x_tile.reshape(2, ni, h_loc, cols, cb).transpose(0, 2, 3, 1, 4)
        yt = fused_block(xt, w_one_part, w_two_part, bias_one.reshape(8, 1, 2 * cb))
        return yt.transpose(0, 3, 1, 2, 4).reshape(x_tile.shape)

    return jax.shard_map(local_block, mesh=mesh, in_specs=(act_spec, kernel_spec, kernel_spec, P()), out_specs=act_spec, check_vma=False)
```

time: 3810 us -> 900 us (0.24)
  waiting for transfers between devices: 2820 us -> 0 us
  Pallas kernels: 0 us -> 874 us
  matrix products: 864 us -> 0 us
  other arithmetic: 61.3 us -> 0 us
    reduce_scatter x2 -> x0, waiting for transfers between devices: 2790 us -> none  [the longest x1 2220 us: local_block(): lax.psum_scatter(part_one, 'cp', scatter_dimension=3, tiled=True)]
    pallas_call x0 -> x1, Pallas kernels: none -> 874 us  [fused_block(): pl.pallas_call(kernel, out_shape=[jax.ShapeDtypeStruct(xt.shape, bf16), j...]
    conv_general_dilated x2 -> x0, matrix products: 864 us -> none  [conv_rows(): lax.conv_general_dilated(padded, kernel, (1, 1), ((0, 0), (1, 1)), dimens...]
    convert_element_type x2 -> x0, other arithmetic: 55.5 us -> none  [the longest x1 43.3 us: local_block(): hidden = jax.nn.relu(summed_one + bias_part).astype(jnp.bfloat16)]
  transfers between devices with their start and end apart: 6 -> 0, of which waited for: 6 -> 0; matrix products, arithmetic and copies ran while one was open for 0% -> 0% of each run, Pallas kernels for 0% -> 0%
where the time goes in v1:
time: 900 us; the launch traced here: 899 us
  Pallas kernels  874 us (97%)
  local copies, waits for them, and re-layouts  25.4 us (3%)
    pallas_call x1, Pallas kernels, fused_block(): pl.pallas_call(kernel, out_shape=[jax.ShapeDtypeStruct(xt.shape, bf16), j...  874 us

profile of v1, /device:TPU:0, one launch (start us, length us, event | category | flops | bytes accessed | tf_op | source)
XLA Modules:
  0.0 899.3 jit_solution(12681461135586134952)
XLA Ops:
  0.0 12.7 %copy.8 = bf16[2,16,48,14,256]{4,1,3,2,0:T(8,128)(2,1)} copy(bf16[2,16,48,14,256]{4,2,3,1,0:T(8,128)(2,1)} %bitcast.8) | data formatting | bytes 22020096 | tf_op jit(solution)/shard_map/reshape | solution.py:516
  12.7 873.9 %fused_block.1 = (bf16[2,48,14,16,256]{4,3,2,1,0:T(8,128)(2,1)}, bf16[3,4,2,3,3,256,512]{6,5,4,3,2,1,0:T(8,128)(2,1)}, bf16[3,2,2,2,3,3,256,512]{7,6,5,4,3,2,1,0...) custom-call(bf16[2,48,14,16,256]{4,3,2,1,0:T(8,128)(2,1)} %bitcast.7, ...), custom_call_target="tpu_custom_call" | custom-call | tf_op jit(solution)/shard_map/fused_block/pallas_call | solution.py:482
  886.7 12.6 %copy.6 = bf16[2,16,48,14,256]{4,2,3,1,0:T(8,128)(2,1)} copy(bf16[2,16,48,14,256]{4,1,3,2,0:T(8,128)(2,1)} %bitcast.9) | data formatting | bytes 22020096 | tf_op jit(solution)/shard_map/transpose | solution.py:518

commit v2 on v1

--- a/solution.py
+++ b/solution.py
@@ -104,14 +104,14 @@
         up_blk = lax.max(blk - 1, 0)
         dn_blk = lax.min(blk + 1, 3)
 
-        def hid_up(q, h):
-            return remote(stage.at[h, 0], hid.at[q, rows + 1], as_.at[0, h], ar.at[1, q], lax.div(up_blk, 2), 2 * x + lax.rem(up_blk, 2))
-
-        def hid_dn(q, h):
-            return remote(stage.at[h, rows - 1], hid.at[q, 0], as_.at[1, h], ar.at[0, q], lax.div(dn_blk, 2), 2 * x + lax.rem(dn_blk, 2))
-
-        def hid_store(q, h):
-            return pltpu.make_async_copy(stage.at[h], hid.at[q, pl.ds(1, rows)], stl.at[h])
+        def hid_up(a):
+            return remote(hid.at[a, 1], hid.at[a, rows + 1], as_.at[0, a], ar.at[1, a], lax.div(up_blk, 2), 2 * x + lax.rem(up_blk, 2))
+
+        def hid_dn(a):
+            return remote(hid.at[a, rows], hid.at[a, 0], as_.at[1, a], ar.at[0, a], lax.div(dn_blk, 2), 2 * x + lax.rem(dn_blk, 2))
+
+        def hid_store(a, h):
+            return pltpu.make_async_copy(stage.at[h], hid.at[a, pl.ds(1, rows)], stl.at[h])
 
         y_rows = pl.ds(rows * c, rows)
 
@@ -127,21 +127,29 @@
         def zero_rows(row):
             return pltpu.make_async_copy(stage.at[0, pl.ds(0, 16)], hid.at[:, row], zsem.at[0])
 
+        def p_of(m):
+            return lax.rem(m + 2, 8)
+
+        def jp(p):
+            return lax.div(p, 2), lax.rem(sp + lax.rem(p, 2), 2)
+
+        def near_step(i):
+            e = lax.rem(i, 4)
+            return 2 * lax.div(i, 4) + lax.rem(e, 2), lax.div(e, 2)
+
+        def halo_wait(role):
+            @pl.when(c != sp)
+            def _():
+                remote(xt.at[0, 0], xa.at[role, 0], hs.at[0], hr.at[role], osp, k).wait_recv()
+
         x_copy(0).start()
-        for xx in range(2):
+        for xx in (x, 1 - x):
             halo_copy(xx).start()
         x_copy(1).start()
-
-        def p_of(m):
-            return lax.rem(m + 2, 8)
-
-        def jp(p):
-            return lax.div(p, 2), lax.rem(sp + lax.rem(p, 2), 2)
-
-        for m in range(3):
+        for m in range(2):
             w1_part(*jp(jnp.int32((m + 2) % 8))).start()
-        for hf in range(2):
-            w1_x(0, hf).start()
+        for e in range(3):
+            w1_x(e // 2, e % 2).start()
 
         stage[0, 0:16] = jnp.zeros((16, cols, ni, cb), jnp.bfloat16)
 
@@ -165,13 +173,14 @@
         def issue(t):
             @pl.when(t < 16)
             def _():
-                j, par = jp(p_of(lax.div(t, 2)))
-
-                @pl.when(lax.rem(t, 2) == 0)
+                m, role = near_step(t)
+                j, par = jp(p_of(m))
+
+                @pl.when(role == 0)
                 def _():
                     w_load(w1_own(j, par, x), t).start()
 
-                @pl.when(lax.rem(t, 2) == 1)
+                @pl.when(role == 1)
                 def _():
                     w1_part(j, par).wait_recv()
                     w_load(g1.at[0, j, par], t).start()
@@ -197,146 +206,192 @@
                 a = 4 * j + 2 * par + h
                 same = lax.rem(j, 2) == c
 
-                @pl.when((n == 0) & (blk > 0))
-                def _():
-                    hid_dn(a, h).wait_recv()
-
-                @pl.when((n == 0) & (blk < 3))
-                def _():
-                    hid_up(a, h).wait_recv()
+                @pl.when(n == 0)
+                def _():
+                    @pl.when(blk > 0)
+                    def _():
+                        hid_dn(a).wait_recv()
+
+                    @pl.when(blk < 3)
+                    def _():
+                        hid_up(a).wait_recv()
 
                 hid_load(a, q).start()
 
-                @pl.when((p < 4) & same)
-                def _():
-                    w_load(w2_cut(n, par, h, x), t).start()
-
-                @pl.when((p < 4) & jnp.logical_not(same))
-                def _():
-                    w2_part(n, par, h).wait_recv()
-                    w_load(g2.at[0, n, par, h], t).start()
-
-                @pl.when((p >= 4) & same)
-                def _():
-                    w_load(g2.at[1, n, par, h], t).start()
-
-                @pl.when((p >= 4) & jnp.logical_not(same))
-                def _():
-                    w2_fwd(n, par, h).wait_recv()
-                    w_load(g2.at[2, n, par, h], t).start()
+                @pl.when(p < 4)
+                def _():
+                    @pl.when(same)
+                    def _():
+                        w_load(w2_cut(n, par, h, x), t).start()
+
+                    @pl.when(jnp.logical_not(same))
+                    def _():
+                        w2_part(n, par, h).wait_recv()
+                        w_load(g2.at[0, n, par, h], t).start()
+
+                @pl.when(p >= 4)
+                def _():
+                    @pl.when(jnp.logical_not(same))
+                    def _():
+                        w2_fwd(n, par, h).wait_recv()
+
+                    w_load(g2.at[jnp.where(same, 1, 2), n, par, h], t).start()
 
         issue(jnp.int32(0))
         x_copy(0).wait()
-
-        @pl.when(c != sp)
-        def _():
-            for role in range(4):
-                remote(xt.at[0, 0], xa.at[role, 0], hs.at[0], hr.at[role], osp, k).wait_recv()
+        halo_wait(0)
+
+        def pass_w1_x(e):
+            j, hf = lax.div(e, 2), lax.rem(e, 2)
+            w1_x(j, hf).wait_recv()
+            w1_y(j, hf).start()
+            w1_fwd(j, sp, hf).start()
+
+        def pass_w1_y(e):
+            j, hf = lax.div(e, 2), lax.rem(e, 2)
+            w1_y(j, hf).wait_recv()
+            w1_fwd(j, osp, hf).start()
+
+        def pass_w2_x(e):
+            n, h = lax.div(e, 2), lax.rem(e, 2)
+            w2_x(n, h).wait_recv()
+            w2_y(n, h).start()
+            w2_fwd(n, sp, h).start()
+
+        def pass_w2_y(e):
+            n, h = lax.div(e, 2), lax.rem(e, 2)
+            w2_y(n, h).wait_recv()
+            w2_fwd(n, osp, h).start()
+
+        def send_w1_x(e):
+            w1_x(lax.div(e, 2), lax.rem(e, 2)).start()
+
+        def send_w2_x(e):
+            w2_x(lax.div(e, 2), lax.rem(e, 2)).start()
 
         def events(i):
-            @pl.when((lax.rem(i, 2) == 0) & (i < 10))
-            def _():
-                w1_part(*jp(p_of(lax.div(i, 2) + 3))).start()
-
-            @pl.when(i == 1)
-            def _():
-                x_copy(1).wait_recv()
-
-            @pl.when(i == 3)
-            def _():
-                x_copy(2).start()
-
-            @pl.when(i == 7)
-            def _():
-                x_copy(3).start()
-
-            @pl.when((i == 13) | (i == 17) | (i == 21))
-            def _():
-                j = lax.div(i - 8, 4)
-                for hf in range(2):
-                    w1_x(j, hf).start()
-
-            @pl.when((i == 24) | (i == 28) | (i == 32) | (i == 36))
-            def _():
-                e = lax.div(i - 24, 4)
-                w2_x(lax.div(e, 2), lax.rem(e, 2)).start()
-
-            @pl.when((i >= 18) & (i < 26))
-            def _():
-                e = i - 18
-                w2_part(lax.div(e, 4), lax.rem(lax.div(e, 2), 2), lax.rem(e, 2)).start()
-
-            @pl.when(i == 6)
-            def _():
-                for hf in range(2):
-                    w1_x(0, hf).wait_recv()
-                    w1_y(0, hf).start()
-                    w1_fwd(0, sp, hf).start()
-
-            @pl.when((i >= 17) & (i < 28) & (lax.rem(i, 2) == 1))
-            def _():
-                e = lax.div(i - 13, 2)
-                j = lax.div(e, 2)
-                hf = lax.rem(e, 2)
-                w1_x(j, hf).wait_recv()
-                w1_y(j, hf).start()
-                w1_fwd(j, sp, hf).start()
-
-            @pl.when((i == 31) | (i == 35) | (i == 39) | (i == 44))
-            def _():
-                e = lax.div(i - 31, 4)
-                w2_x(lax.div(e, 2), lax.rem(e, 2)).wait_recv()
-                w2_y(lax.div(e, 2), lax.rem(e, 2)).start()
-                w2_fwd(lax.div(e, 2), sp, lax.rem(e, 2)).start()
-
-            @pl.when(i == 11)
-            def _():
-                for hf in range(2):
-                    w1_y(0, hf).wait_recv()
-                    w1_fwd(0, osp, hf).start()
-
-            @pl.when((i == 20) | (i == 24) | (i == 28))
-            def _():
-                j = lax.div(i - 16, 4)
-                w1_y(j, 0).wait_recv()
-                w1_fwd(j, osp, 0).start()
-
-            @pl.when((i == 21) | (i == 25) | (i == 29))
-            def _():
-                j = lax.div(i - 17, 4)
-                w1_y(j, 1).wait_recv()
-                w1_fwd(j, osp, 1).start()
-
-            @pl.when((i == 36) | (i == 40) | (i == 45) | (i == 49))
-            def _():
-                e = lax.div(i - 36, 4)
-                w2_y(lax.div(e, 2), lax.rem(e, 2)).wait_recv()
-                w2_fwd(lax.div(e, 2), osp, lax.rem(e, 2)).start()
-
-            stored = (i >= 19) & (i <= 33) & (lax.rem(i, 2) == 1)
-
-            @pl.when(stored)
-            def _():
-                for h in range(2):
-                    hid_store(0, h).wait()
-
-            @pl.when(stored & (blk > 0))
-            def _():
-                for h in range(2):
-                    hid_up(0, h).wait_send()
-
-            @pl.when(stored & (blk < 3))
-            def _():
-                for h in range(2):
-                    hid_dn(0, h).wait_send()
-
-            @pl.when(i == 16)
-            def _():
-                x_copy(2).wait_recv()
-
-            @pl.when(i == 17)
-            def _():
-                x_copy(3).wait_recv()
+            even = lax.rem(i, 2) == 0
+            odd = jnp.logical_not(even)
+
+            @pl.when(i < 16)
+            def _():
+                @pl.when(even)
+                def _():
+                    @pl.when(i < 12)
+                    def _():
+                        w1_part(*jp(p_of(lax.div(i, 2) + 2))).start()
+
+                    @pl.when(i == 2)
+                    def _():
+                        x_copy(1).wait_recv()
+                        halo_wait(1)
+
+                    @pl.when(i == 4)
+                    def _():
+                        x_copy(2).start()
+
+                    @pl.when(i == 10)
+                    def _():
+                        for e in range(2):
+                            pass_w1_y(jnp.int32(e))
+
+                    @pl.when(i == 12)
+                    def _():
+                        pass_w1_y(jnp.int32(2))
+
+                @pl.when(odd)
+                def _():
+                    @pl.when(i == 5)
+                    def _():
+                        for e in range(2):
+                            pass_w1_x(jnp.int32(e))
+
+                    @pl.when(i == 7)
+                    def _():
+                        pass_w1_x(jnp.int32(2))
+
+                    @pl.when(i == 9)
+                    def _():
+                        x_copy(3).start()
+
+                    @pl.when(i >= 13)
+                    def _():
+                        send_w1_x(lax.div(i - 7, 2))
+
+            @pl.when((i >= 16) & (i < 34))
+            def _():
+                @pl.when(i < 24)
+                def _():
+                    e = i - 16
+                    w2_part(lax.div(e, 4), lax.rem(lax.div(e, 2), 2), lax.rem(e, 2)).start()
+
+                @pl.when(even)
+                def _():
+                    @pl.when(i == 16)
+                    def _():
+                        x_copy(2).wait_recv()
+                        halo_wait(2)
+
+                    @pl.when((i >= 24) & (lax.rem(i, 4) == 0))
+                    def _():
+                        send_w2_x(lax.div(i - 24, 4))
+
+                    @pl.when((i >= 18) & (i <= 26))
+                    def _():
+                        pass_w1_x(lax.div(i - 12, 2))
+
+                @pl.when(odd)
+                def _():
+                    @pl.when(i == 17)
+                    def _():
+                        x_copy(3).wait_recv()
+                        halo_wait(3)
+
+                    @pl.when(i <= 21)
+                    def _():
+                        send_w1_x(lax.div(i - 7, 2))
+
+                    @pl.when(i >= 19)
+                    def _():
+                        for h in range(2):
+                            hid_store(0, h).wait()
+
+                    @pl.when((i >= 21) & (i <= 29))
+                    def _():
+                        pass_w1_y(lax.div(i - 15, 2))
+
+                    @pl.when(i >= 27)
+                    def _():
+                        for d in range(2):
+                            j, par = jp(i - 27 + d)
+                            for h in range(2):
+                                a = 4 * j + 2 * par + h
+
+                                @pl.when(blk > 0)
+                                def _():
+                                    hid_up(a).start()
+
+                                @pl.when(blk < 3)
+                                def _():
+                                    hid_dn(a).start()
+
+                    @pl.when(i == 31)
+                    def _():
+                        pass_w2_x(jnp.int32(0))
+
+            @pl.when((i >= 34) & (i < 50))
+            def _():
+                @pl.when(i == 36)
+                def _():
+                    send_w2_x(jnp.int32(3))
+
+                @pl.when((i < 44) & (lax.rem(i, 4) == 3))
+                def _():
+                    pass_w2_x(lax.div(i - 31, 4))
+
+                @pl.when((i >= 37) & (lax.rem(i, 4) == 1))
+                def _():
+                    pass_w2_y(lax.div(i - 37, 4))
 
         def taps(xs_slot, ws_slot, col):
             total = None
@@ -350,16 +405,19 @@
             return total
 
         def step(i, carry):
+            ph1 = i < 16
             ph3 = i >= 32
-            odd = lax.rem(i, 2) == 1
             n = jnp.where(ph3, lax.div(i - 32, 16), 0)
             q = jnp.where(ph3, lax.rem(i - 32, 16), 0)
-            m = lax.div(i, 2)
-            p = jnp.where(i < 16, p_of(m), lax.rem(m, 8))
-            last = jnp.where(ph3, q == 15, (i >= 16) & odd)
-            first = jnp.where(ph3, q == 0, (i < 16) & jnp.logical_not(odd))
+            m, role = near_step(i)
+            m = jnp.where(ph1, m, lax.div(i - 16, 2))
+            role = jnp.where(ph1, role, 2 + lax.rem(i, 2))
+            p = jnp.where(ph1, p_of(m), lax.rem(m, 8))
+            p = jnp.where(ph3, 0, p)
+            last = jnp.where(ph3, q == 15, role == 3)
+            first = jnp.where(ph3, q == 0, role == 0)
             a_slot = jnp.where(ph3, n, lax.rem(p, 2))
-            x_slot = jnp.where(ph3, 4 + lax.rem(q, 2), jnp.where(i < 16, 0, 2) + lax.rem(i, 2))
+            x_slot = jnp.where(ph3, 4 + lax.rem(q, 2), role)
             w_slot = lax.rem(i, 2)
 
             events(i)
@@ -370,13 +428,15 @@
             def _():
                 hid_load(0, q).wait()
 
-            @pl.when((i >= 4) & (i < 16) & jnp.logical_not(odd))
-            def _():
-                pltpu.make_async_copy(acc.at[a_slot], part.at[0], pst.at[a_slot]).wait()
-
-            @pl.when((i >= 20) & (i < 32) & jnp.logical_not(odd))
-            def _():
-                pltpu.make_async_copy(part.at[0], acc.at[a_slot], pld.at[a_slot]).wait()
+            @pl.when((i >= 4) & (i < 32))
+            def _():
+                @pl.when(ph1 & first)
+                def _():
+                    pltpu.make_async_copy(acc.at[a_slot], part.at[0], pst.at[a_slot]).wait()
+
+                @pl.when((i >= 20) & (role == 2))
+                def _():
+                    pltpu.make_async_copy(part.at[0], acc.at[a_slot], pld.at[a_slot]).wait()
 
             @pl.when(jnp.logical_not(last))
             def _():
@@ -384,7 +444,7 @@
                     total = taps(x_slot, w_slot, col)
                     acc[a_slot, col] = total + jnp.where(first, 0.0, acc[a_slot, col])
 
-            @pl.when((i < 12) & odd)
+            @pl.when((i < 12) & (role == 1))
             def _():
                 pltpu.make_async_copy(acc.at[a_slot], part.at[p], pst.at[a_slot]).start()
 
@@ -414,19 +474,8 @@
 
                 @pl.when(i < 32)
                 def _():
-                    a = 4 * j + 2 * par
                     for h in range(2):
-                        hid_store(a + h, h).start()
-
-                    @pl.when(blk > 0)
-                    def _():
-                        for h in range(2):
-                            hid_up(a + h, h).start()
-
-                    @pl.when(blk < 3)
-                    def _():
-                        for h in range(2):
-                            hid_dn(a + h, h).start()
+                        hid_store(4 * j + 2 * par + h, h).start()
 
                     @pl.when(p < 6)
                     def _():
@@ -464,6 +513,19 @@
             return carry
 
         lax.fori_loop(0, 8, drain, 0)
+
+        def drain_rows(a, carry):
+            @pl.when(blk > 0)
+            def _():
+                hid_up(a).wait_send()
+
+            @pl.when(blk < 3)
+            def _():
+                hid_dn(a).wait_send()
+
+            return carry
+
+        lax.fori_loop(0, 16, drain_rows, 0)
 
         def drain_two(e, carry):
             w2_x(lax.div(e, 2), lax.rem(e, 2)).wait_send()
@@ -498,7 +560,7 @@
             dma((2,)), dma((2,)), dma((2,)), dma((2,)), dma((2,)), dma((1,)), dma((1,)), dma((3,)), dma((3,)), dma((2,)), dma((4,)),
             dma((4, 2)), dma((4, 2)), dma((4, 2)), dma((4, 2)), dma((4, 2)), dma((4, 2)), dma((4, 2, 2)), dma((4, 2, 2)),
             dma((2, 2, 2)), dma((2, 2, 2)), dma((2, 2)), dma((2, 2)), dma((2, 2)), dma((2, 2)), dma((2, 2, 2)), dma((2, 2, 2)),
-            dma((2, 2)), dma((2, 16)), dma((2,)), dma((2,)), dma((1,)), dma((1,)), dma((1,)),
+            dma((2, 16)), dma((2, 16)), dma((2,)), dma((2,)), dma((1,)), dma((1,)), dma((1,)),
         ],
         compiler_params=pltpu.CompilerParams(collective_id=0, has_side_effects=True, vmem_limit_bytes=60 * 1024 * 1024),
         name="fused_block",

time: 900 us -> 846 us (0.940)
  Pallas kernels: 874 us -> 820 us
    pallas_call x1, Pallas kernels: 874 us -> 820 us  [fused_block(): pl.pallas_call(kernel, out_shape=[jax.ShapeDtypeStruct(xt.shape, bf16), j...]
where the time goes in v2:
time: 846 us
  Pallas kernels  820 us (97%)
  local copies, waits for them, and re-layouts  25.4 us (3%)
    pallas_call x1, Pallas kernels, fused_block(): pl.pallas_call(kernel, out_shape=[jax.ShapeDtypeStruct(xt.shape, bf16), j...  820 us

profile of v2, /device:TPU:0, one launch (start us, length us, event | category | flops | bytes accessed | tf_op | source)
XLA Modules:
  0.0 845.7 jit_solution(17139760360838786146)
XLA Ops:
  0.0 12.7 %copy.8 = bf16[2,16,48,14,256]{4,1,3,2,0:T(8,128)(2,1)} copy(bf16[2,16,48,14,256]{4,2,3,1,0:T(8,128)(2,1)} %bitcast.8) | data formatting | bytes 22020096 | tf_op jit(solution)/shard_map/reshape | solution.py:578
  12.7 820.3 %fused_block.1 = (bf16[2,48,14,16,256]{4,3,2,1,0:T(8,128)(2,1)}, bf16[3,4,2,3,3,256,512]{6,5,4,3,2,1,0:T(8,128)(2,1)}, bf16[3,2,2,2,3,3,256,512]{7,6,5,4,3,2,1,0...) custom-call(bf16[2,48,14,16,256]{4,3,2,1,0:T(8,128)(2,1)} %bitcast.7, ...), custom_call_target="tpu_custom_call" | custom-call | tf_op jit(solution)/shard_map/fused_block/pallas_call | solution.py:544
  833.0 12.6 %copy.6 = bf16[2,16,48,14,256]{4,2,3,1,0:T(8,128)(2,1)} copy(bf16[2,16,48,14,256]{4,1,3,2,0:T(8,128)(2,1)} %bitcast.9) | data formatting | bytes 22020096 | tf_op jit(solution)/shard_map/transpose | solution.py:580
